TPU v7x, 32 devices: a whole 2x2x4 slice. The times are simulated.
32 devices in a mesh: wa: 8 (over y, x, core), ch: 4 (over z).
Axes of the slice: x: 2, y: 2, z: 4, core: 2. Of those that a mesh axis runs over, the one named last changes fastest.
Arguments:
- grid_cells: int32 [2, 16384], P(None, ('wa', 'ch')), may hold values from -4096 to 4095
- visibilities: float32 [2, 16384], P(None, ('wa', 'ch')), may hold values from -6 to 6
- weights: float32 [16384], P(('wa', 'ch')), may hold values from 0.25 to 4
- layer_index: int32 [16384], P(('wa', 'ch')), may hold values from 0 to 7, as said below
- group_index: int32 [16384], P(('wa', 'ch')), may hold values from 0 to 3, as said below
- plane_depths: float32 [8], P('wa'), may hold values from -1000 to 1000
- sky_model: float32 [4, 128, 4096], P('ch', 'wa'), may hold values from -6 to 6
Outputs:
- residual: float32 [4, 128, 4096], P('ch', 'wa')
Inputs may be any that keep to these rules, and one draw needn't show every extreme that they name: `layer_index`: among the 512 visibilities of one device, at most 32 have the same layer and the same group; one layer and group has exactly 32 on every device. `group_index`: drawn together with layer_index.
All inputs are finite; a program needn't handle non-finite values.
Results may differ from a plain program's by a relative error of at most 0.0026.
Values sent between devices are 32-bit elements; how exact they have to be, the bound alone decides.
A program may use at most 128 MiB of HBM per device.

v0:
```python
import math

import jax
import jax.numpy as jnp
from jax import lax
from jax.sharding import PartitionSpec as P

GRID = 8192


def phase_table(left, right, grid_size):
    product = jnp.mod(left[:, None] * right[None, :], grid_size)
    return product.astype(jnp.float32) * (2.0 * math.pi / grid_size)


def column_factor(real_part, imag_part, weight, column_cells, columns, grid_size):
    pixels = jnp.arange(columns, dtype=jnp.int32) - columns // 2 + grid_size // 8
    angles = phase_table(column_cells, pixels, grid_size)
    weighted_real = weight * real_part
    weighted_imag = weight * imag_part
    cosines = jnp.cos(angles)
    sine_values = jnp.sin(angles)
    column_real = (weighted_real[:, None] * cosines - weighted_imag[:, None] * sine_values).astype(
        jnp.bfloat16
    )
    column_imag = (weighted_real[:, None] * sine_values + weighted_imag[:, None] * cosines).astype(
        jnp.bfloat16
    )
    return jnp.concatenate([column_real, column_imag], 0)


def row_factor(row_cells, row_count, total_rows, grid_size):
    pixels = jnp.arange(row_count, dtype=jnp.int32) - total_rows // 2 + grid_size // 8
    angles = phase_table(pixels, row_cells, grid_size)
    real_part = jnp.cos(angles).astype(jnp.bfloat16)
    imag_part = jnp.sin(angles).astype(jnp.bfloat16)
    upper_half = jnp.concatenate([real_part, -imag_part], 1)
    lower_half = jnp.concatenate([imag_part, real_part], 1)
    return jnp.concatenate([upper_half, lower_half], 0)


def layer_image(row_factors, column_factors, w_value, row_count, total_rows, columns, grid_size):
    product = jnp.dot(row_factors, column_factors, preferred_element_type=jnp.float32)
    real_sum = product[:row_count]
    imag_sum = product[row_count:]
    row_pixels = jnp.arange(row_count, dtype=jnp.int32) - total_rows // 2 + grid_size // 8
    column_pixels = jnp.arange(columns, dtype=jnp.int32) - columns // 2 + grid_size // 8
    row_cosine = 0.8 * row_pixels.astype(jnp.float32) / grid_size
    column_cosine = 0.8 * column_pixels.astype(jnp.float32) / grid_size
    depth_term = jnp.sqrt(1.0 - row_cosine[:, None] ** 2 - column_cosine[None, :] ** 2) - 1.0
    screen = 2.0 * math.pi * w_value * depth_term
    return jnp.cos(screen) * real_sum - jnp.sin(screen) * imag_sum


def on_device(grid_cells, visibilities, weights, layer_index, group_index, plane_depths, sky_model):
    layer_count = lax.axis_size("wa")
    groups = lax.axis_size("ch")
    dest_count = layer_count * groups
    held = weights.shape[0]
    capacity = 2 * held // dest_count
    rows_dev = sky_model.shape[1]
    columns = sky_model.shape[2]
    total_rows = rows_dev * layer_count
    target = layer_index * groups + group_index
    onehot = (target[:, None] == jnp.arange(dest_count, dtype=jnp.int32)[None, :]).astype(jnp.int32)
    before = jnp.cumsum(onehot, 0) - onehot
    slot_rank = jnp.sum(before * onehot, 1)
    slot_index = target * capacity + slot_rank
    payload = jnp.stack(
        [
            visibilities[0],
            visibilities[1],
            weights,
            grid_cells[0].astype(jnp.float32),
            grid_cells[1].astype(jnp.float32),
        ],
        0,
    )
    outgoing = jnp.zeros((5, dest_count * capacity), jnp.float32).at[:, slot_index].set(payload)
    arrived = lax.all_to_all(
        outgoing.reshape(5, dest_count, capacity),
        ("wa", "ch"),
        split_axis=1,
        concat_axis=1,
        tiled=True,
    )
    received = arrived.reshape(5, dest_count * capacity)
    noise_power = lax.psum(jnp.sum(received[2] * received[2]), "wa")
    row_cells = received[3].astype(jnp.int32)
    column_cells = received[4].astype(jnp.int32)
    column_factors = column_factor(
        received[0], received[1], received[2], column_cells, columns, GRID
    )
    row_factors = row_factor(row_cells, rows_dev * lax.axis_size("wa"), total_rows, GRID)
    dirty_tile = lax.psum_scatter(
        layer_image(
            row_factors,
            column_factors,
            plane_depths[0],
            rows_dev * lax.axis_size("wa"),
            total_rows,
            columns,
            GRID,
        ),
        "wa",
        scatter_dimension=0,
        tiled=True,
    )
    return (dirty_tile * lax.rsqrt(noise_power) - sky_model[0])[None]


def solution(mesh):
    return jax.shard_map(
        on_device,
        mesh=mesh,
        in_specs=(
            P(None, ("wa", "ch")),
            P(None, ("wa", "ch")),
            P(("wa", "ch")),
            P(("wa", "ch")),
            P(("wa", "ch")),
            P("wa"),
            P("ch", "wa", None),
        ),
        out_specs=P("ch", "wa", None),
        check_vma=False,
    )
```

profile of v0, /device:TPU:0, one launch (start us, length us, event | category | flops | bytes accessed | tf_op | source)
XLA Modules:
  0.0 169.2 jit_solution(3066334894558804468)
XLA Ops:
  6.5 0.7 multiply_add_fusion
  7.2 1.2 reduce-window.6
  8.4 0.2 slice_reduce_fusion
  8.7 0.1 fusion.25
  8.8 0.8 slice_convert_fusion.3
  9.6 0.7 maximum_bitcast_fusion
  10.3 0.1 copy.13
  10.4 1.8 %scatter_custom_fusion = f32[5,1024]{0,1:T(8,128)S(1)} fusion(s32[512]{0:T(512)S(1)} %compare_select_fusion, f32[512,5]{1,0:T(8,128)S(1)} %copy.13, f32[]{:T(128)} %constant.60.clone.1), kind=kCustom, calls=%fused_computation.39 | custom fusion | bytes 20484 | tf_op jit(solution)/shard_map/scatter | solution.py:79
  12.3 0.3 copy.14
  12.6 0.7 reshape.124
  13.3 7.3 %all-to-all-start = ((f32[32,1,160]{2,1,0:T(1,128)}), f32[32,1,160]{2,1,0:T(1,128)S(1)}, u32[]{:S(2)}, u32[]{:S(2)}) async-start(f32[32,1,160]{2,1,0:T(1,128)} %reshape.124), calls=%async_computation | async-start | bytes 65536 | tf_op jit(solution)/shard_map/all_to_all | solution.py:80
  21.4 6.6 %all-to-all-done = f32[32,1,160]{2,1,0:T(1,128)S(1)} async-done(((f32[32,1,160]{2,1,0:T(1,128)}), f32[32,1,160]{2,1,0:T(1,128)S(1)}, u32[]{:S(2)}, u32[]{:S(2)}) %all-to-all-start) | async-done | bytes 20512 | tf_op jit(solution)/shard_map/all_to_all | solution.py:80
  27.9 0.5 broadcast.117
  28.4 0.7 reduce.19
  29.2 0.7 multiply_reduce_fusion
  30.0 0.1 fusion.31
  30.1 2.4 %sine_convert_fusion = (bf16[128,1024]{1,0:T(8,128)(2,1)S(1)}, bf16[128,1024]{1,0:T(8,128)(2,1)S(1)}) fusion(s32[1024]{0:T(1024)S(1)} %convert_element_type.74, s32[128]{0:T(128)S(1)} %iota_add_fusion.1), kind=kLoop, calls=%fused_computation.35 | loop fusion | flops 2097152 | bytes 528896 | tf_op jit(solution)/shard_map/convert_element_type | solution.py:36
  32.6 2.1 %fusion.27 = bf16[128,1024]{1,0:T(8,128)(2,1)S(1)} fusion(s32[1024]{0:T(1024)S(1)} %convert_element_type.74, s32[128]{0:T(128)S(1)} %iota_add_fusion.1), kind=kLoop, calls=%fused_computation.50 | loop fusion | flops 2359296 | bytes 266752 | tf_op jit(solution)/shard_map/neg | solution.py:37
  34.9 71.5 %subtract_convert_fusion = (bf16[1024,4096]{1,0:T(8,128)(2,1)S(1)}, bf16[1024,4096]{1,0:T(8,128)(2,1)}) fusion(f32[1024]{0:T(1024)S(1)} %mul.151, s32[4096]{0:T(1024)S(1)} %iota_add_fusion, s32[1024]{0:T(1024)S(1)} %convert_element_type.79, f32[1024]{0:T(1024)S(1)} %mul.142), kind=kLoop, calls=%fused_computation.14 | loop fusion | flops 92274688 | bytes 16805888 | tf_op jit(solution)/shard_map/convert_element_type | solution.py:23
  106.4 7.0 %fusion.3 = f32[256,4096]{1,0:T(8,128)S(1)} fusion(bf16[1024,4096]{1,0:T(8,128)(2,1)} %get-tuple-element.11, bf16[1024,4096]{1,0:T(8,128)(2,1)S(1)} %get-tuple-element.10, bf16[128,1024]{1,0:T(8,128)(2,1)S(1)} %get-tuple-element.13, bf16[128,1024]{1,0:T(8,128)(2,1)S(1)} %get-tuple-element.12, bf16[128,1024]{1,0:T(8,128)(2,1)S(1)} %fusion.27), kind=kOutput, calls=%fused_computation.9 | convolution fusion | flops 4332716032 | bytes 21757952 | tf_op jit(solution)/shard_map/dot_general | solution.py:43
  113.4 9.6 %fusion.9 = f32[128,4096]{1,0:T(8,128)} fusion(f32[256,4096]{1,0:T(8,128)S(1)} %fusion.3, f32[4096]{0:T(1024)S(1)} %multiply_multiply_fusion, f32[128]{0:T(128)S(1)} %multiply_subtract_fusion, f32[]{:T(128)} %bitcast), kind=kLoop, calls=%fused_computation.18 | loop fusion | flops 3145728 | bytes 6308356 | tf_op jit(solution)/shard_map/sub | solution.py:52
  123.0 12.6 %psum.7 = f32[]{:T(128)} all-reduce(f32[]{:T(128)} %get-tuple-element.5), channel_id=1, replica_groups=mesh['wa'=8,'ch'=4] {'wa'}, use_global_device_ids=true, to_apply=%region_6.7 | all-reduce | flops 1 | bytes 8 | tf_op jit(solution)/shard_map/psum | solution.py:88
  136.3 24.4 %reduce-scatter.2.cloned.1.call-done = f32[16,4096]{1,0:T(8,128)} async-done(((f32[128,4096]{1,0:T(8,128)}), f32[16,4096]{1,0:T(8,128)}) %reduce-scatter.2.cloned.1.call-update) | async-done | bytes 262160 | tf_op jit(solution)/shard_map/reduce_scatter | solution.py:95
  160.7 1.7 fusion.20
  (17 shorter events, 0.5 us)
Async XLA Ops:
  13.3 14.6 %all-to-all-start = ((f32[32,1,160]{2,1,0:T(1,128)}), f32[32,1,160]{2,1,0:T(1,128)S(1)}, u32[]{:S(2)}, u32[]{:S(2)}) async-start(f32[32,1,160]{2,1,0:T(1,128)} %reshape.124), calls=%async_computation | async-start | bytes 65536 | tf_op jit(solution)/shard_map/all_to_all | solution.py:80
  20.6 140.1 %reduce-scatter.2.cloned.1.call-start = ((), (), s32[]{:S(2)}) async-start(), calls=%async_computation.2 | async-start | bytes 2359296 | tf_op jit(solution)/shard_map/reduce_scatter | solution.py:95
  113.4 47.3 %copy-start = (f32[1,16,4096]{2,1,0:T(8,128)S(1)}, f32[1,16,4096]{2,1,0:T(8,128)}, u32[]{:S(2)}) copy-start(f32[1,16,4096]{2,1,0:T(8,128)} %param.13) | copy-start | bytes 786436
Sparse Core Ops, SparseCore 0:
  123.1 37.4 reduce-scatter.1
where the time goes:
time: 170 us; the launch traced here: 169 us
  other arithmetic  92.4 us (54%)
  waiting for transfers between devices  31 us (18%)
  between operations  14.8 us (9%)
  blocking collectives  12.6 us (7%)
  starting transfers between devices  7.37 us (4%)
  matrix products  6.98 us (4%)
  local copies, waits for them, and re-layouts  4.08 us (2%)
    convert_element_type x1, other arithmetic, column_factor(): (weighted_real[:, None] * cosines - weighted_imag[:, None] * sine_values)...  71.5 us
    reduce_scatter x1, waiting for transfers between devices, on_device(): lax.psum_scatter(layer_image(row_factors, column_factors, plane_depths[0]...  24.4 us
    psum x1, blocking collectives, on_device(): noise_power = lax.psum(jnp.sum(received[2] * received[2]), 'wa')  12.6 us
    sub x1, other arithmetic, layer_image(): return jnp.cos(screen) * real_sum - jnp.sin(screen) * imag_sum  9.59 us
    all_to_all x1, starting transfers between devices, on_device(): lax.all_to_all(outgoing.reshape(5, dest_count, capacity), ('wa', 'ch'), s...  7.33 us
    dot_general x1, matrix products, layer_image(): jnp.dot(row_factors, column_factors, preferred_element_type=jnp.float32)  6.98 us
    all_to_all x1, waiting for transfers between devices, on_device(): lax.all_to_all(outgoing.reshape(5, dest_count, capacity), ('wa', 'ch'), s...  6.55 us
  transfers between devices with their start and end apart: 2, of which 2 were waited for; matrix products, arithmetic and copies ran while one was open for 0% of the time, Pallas kernels for 0%

commit v1 on v0

v1 whole, which is shorter than its diff:
```python
import functools

import jax
import jax.numpy as jnp
from jax import lax
from jax.experimental import pallas as pl
from jax.experimental.pallas import tpu as pltpu
from jax.sharding import PartitionSpec as P

GRID = 8192
MESH = pl.DeviceIdType.MESH
SIN = (3.1415926400772034, -5.167710076668359, 2.5500773865296704, -0.5982904112879445, 0.07765591228493303)
COS = (0.9999999530275129, -4.934792802489486, 4.058410790762989, -1.3318729727896825, 0.21968242357961013)
F32 = jnp.float32
BF16 = jnp.bfloat16


def sincos(turns):
    y = turns * turns
    s = SIN[4]
    c = COS[4]
    for k in (3, 2, 1, 0):
        s = s * y + SIN[k]
        c = c * y + COS[k]
    s = s * turns
    s2 = s + s
    return s2 * c, 1.0 - s2 * s


def unit(phase):
    wrapped = ((phase + GRID) & (2 * GRID - 1)) - GRID
    return sincos(wrapped.astype(F32) * (0.5 / GRID))


def split3(x):
    high = x.astype(BF16)
    rest = x - high.astype(F32)
    mid = rest.astype(BF16)
    low = (rest - mid.astype(F32)).astype(BF16)
    return high, mid, low


def dot_nt(left, right):
    return lax.dot_general(left, right, (((1,), (1,)), ((), ())), preferred_element_type=F32)


def dot_nn(left, right):
    return jnp.dot(left, right, preferred_element_type=F32)


def exchange(axis, count, send_sem, recv_sem, source, target):
    me = lax.axis_index(axis)
    copies = []
    for step in range(1, count):
        to = lax.rem(me + step, count)
        copy = pltpu.make_async_remote_copy(
            src_ref=source(to),
            dst_ref=target(me),
            send_sem=send_sem.at[step],
            recv_sem=recv_sem.at[step],
            device_id={axis: to},
            device_id_type=MESH,
        )
        copy.start()
        copies.append(copy)
    return copies


def kernel(
    sizes, pay_ref, sky_ref, out_ref, msg, got, gathered, depth, a_ref, b_ref, x_ref, acc, outb, land,
    send1, recv1, send2, recv2, send3, recv3,
):
    n_wa, n_ch, cap, rows, rows_dev, columns = sizes
    layers = n_wa
    cols = columns // n_wa
    half_c, half_r = cols // 2, rows // 2
    held = pay_ref.shape[1]
    dests = n_wa * n_ch
    width = layers * cap
    me_wa, me_ch = lax.axis_index("wa"), lax.axis_index("ch")

    barrier = pltpu.get_barrier_semaphore()
    for axis, count, me in (("wa", n_wa, me_wa), ("ch", n_ch, me_ch)):
        for step in range(1, count):
            pl.semaphore_signal(
                barrier, inc=1, device_id={axis: lax.rem(me + step, count)}, device_id_type=MESH
            )

    payload = pay_ref[...]
    target = payload[5:6, :] * float(layers) + payload[6:7, :]
    onehot = lax.broadcasted_iota(jnp.int32, (dests, held), 0).astype(F32) == target
    earlier = (
        lax.broadcasted_iota(jnp.int32, (held, held), 0)
        < lax.broadcasted_iota(jnp.int32, (held, held), 1)
    )
    before = dot_nn(
        jnp.where(onehot, 1.0, 0.0).astype(BF16), jnp.where(earlier, 1.0, 0.0).astype(BF16)
    )
    rank = jnp.sum(jnp.where(onehot, before, 0.0), 0, keepdims=True)
    slot = target * float(cap) + rank
    parts = split3(payload)
    for group in range(n_ch):
        numbers = lax.broadcasted_iota(jnp.int32, (width, held), 0) + group * width
        select = jnp.where(numbers.astype(F32) == slot, 1.0, 0.0).astype(BF16)
        high, mid, low = (dot_nt(part, select) for part in parts)
        msg[group] = (high + mid) + low

    pl.semaphore_wait(barrier, n_wa + n_ch - 2)
    copies = exchange("ch", n_ch, send1, recv1, lambda to: msg.at[to], lambda me: got.at[me])
    got[me_ch] = msg[me_ch]

    left = me_wa * cols - columns // 2 + GRID // 8 + half_c
    top = GRID // 8

    @pl.loop(0, half_r // 8)
    def _(i):
        p = lax.broadcasted_iota(jnp.int32, (8, half_c), 0) + i * 8
        q = lax.broadcasted_iota(jnp.int32, (8, half_c), 1)
        for s1 in range(2):
            for s2 in range(2):
                l_pix = top + p if s1 == 0 else top - 1 - p
                m_pix = left + q if s2 == 0 else left - 1 - q
                l = 0.8 * l_pix.astype(F32) / GRID
                m = 0.8 * m_pix.astype(F32) / GRID
                s = l * l + m * m
                depth[2 * s1 + s2, pl.ds(i * 8, 8), :] = -s / (1.0 + jnp.sqrt(1.0 - s))
                acc[2 * s1 + s2, pl.ds(i * 8, 8), :] = jnp.zeros((8, half_c), F32)

    for copy in copies:
        copy.wait()

    lane = lax.broadcasted_iota(jnp.int32, (8, 128), 1)
    sub = lax.broadcasted_iota(jnp.int32, (8, 128), 0)

    def packed(layer):
        tile = jnp.zeros((8, 128), F32)
        at = layer * cap
        for c in range(n_ch):
            piece = got[c, :, at // 128 * 128 : at // 128 * 128 + 128]
            shift = (c * cap - at) % 128
            if shift:
                piece = pltpu.roll(piece, shift, 1)
            tile = jnp.where((lane >= c * cap) & (lane < (c + 1) * cap), piece, tile)
        return tile

    for pair in range(layers // 2):
        odd = pltpu.roll(packed(2 * pair + 1), 4, 0)
        gathered[me_wa, pair] = jnp.where(sub < 4, packed(2 * pair), odd)
    power = jnp.zeros((1, width), F32)
    for c in range(n_ch):
        weight = got[c, 4:5, :]
        power = power + weight * weight
    power = jnp.sum(power, 1, keepdims=True)
    gathered[me_wa, layers // 2] = jnp.where(sub == 0, payload[7:8, :128], jnp.where(sub == 1, power, 0.0))

    mine = gathered.at[me_wa]
    copies = exchange("wa", n_wa, send2, recv2, lambda to: mine, lambda me: gathered.at[me])
    for copy in copies:
        copy.wait()

    center_r = 2 * (GRID // 8) - 1
    center_c = 2 * left - 1
    f_iota = lax.broadcasted_iota(jnp.int32, (16, 128), 0) * 2 + 1

    def layer_step(pair, parity):
        @pl.loop(0, n_wa)
        def _(block):
            lanes = pl.ds(pl.multiple_of(block * 128, 128), 128)
            base = 4 * parity
            zr, zi = (gathered[block, pair, base + k : base + k + 1, :] for k in (0, 1))
            u, v = (gathered[block, pair, base + k : base + k + 1, :].astype(jnp.int32) for k in (2, 3))
            sc, cc = unit(u * center_r + v * center_c)
            wr, wi = zr * cc - zi * sc, zr * sc + zi * cc
            wr, wi = jnp.broadcast_to(wr, (16, 128)), jnp.broadcast_to(wi, (16, 128))
            for cell, half in ((u, half_r), (v, half_c)):
                fs, fc = unit(cell * f_iota)
                coarse = max(half // 16, 8)
                steps = lax.broadcasted_iota(jnp.int32, (coarse, 128), 0) * 32
                es, ec = unit(cell * steps)
                for a in range(half // 16):
                    e_s, e_c = es[a : a + 1, :], ec[a : a + 1, :]
                    c = e_c * fc - e_s * fs
                    s = e_s * fc + e_c * fs
                    if cell is u:
                        for k, term in enumerate((wr * c, wr * s, wi * c, wi * s)):
                            a_ref[k * half + 16 * a : k * half + 16 * a + 16, lanes] = term.astype(BF16)
                    else:
                        for k, term in enumerate((c, s)):
                            b_ref[k * half + 16 * a : k * half + 16 * a + 16, lanes] = term.astype(BF16)

        deep = min(1024, n_wa * 128)

        @pl.loop(0, 4 * half_r // 256)
        def _(i):
            tall = pl.ds(pl.multiple_of(i * 256, 256), 256)
            if n_wa * 128 == deep:
                x_ref[tall, :] = dot_nt(a_ref[tall, :], b_ref[...])
            else:
                x_ref[tall, :] = jnp.zeros((256, cols), F32)

                @pl.loop(0, n_wa * 128 // deep)
                def _(k):
                    inner = pl.ds(pl.multiple_of(k * deep, deep), deep)
                    x_ref[tall, :] += dot_nt(a_ref[tall, inner], b_ref[:, inner])

        w = gathered[2 * pair + parity, layers // 2, 0:1, 0:1]

        @pl.loop(0, half_r // 8)
        def _(i):
            x = [
                [
                    x_ref[pl.ds(pl.multiple_of(k * half_r + i * 8, 8), 8), g * half_c : (g + 1) * half_c]
                    for g in range(2)
                ]
                for k in range(4)
            ]
            (rcc, rcs), (rsc, rss), (icc, ics), (isc, iss) = x
            same_r, cross_r = (rcc - rss, rcc + rss), (isc + ics, isc - ics)
            same_i, cross_i = (icc - iss, icc + iss), (rsc + rcs, rsc - rcs)
            for s1 in range(2):
                for s2 in range(2):
                    k = 0 if s1 == s2 else 1
                    if s1 == 0:
                        real, imag = same_r[k] - cross_r[k], same_i[k] + cross_i[k]
                    else:
                        real, imag = same_r[k] + cross_r[k], same_i[k] - cross_i[k]
                    at = pl.ds(pl.multiple_of(i * 8, 8), 8)
                    turns = depth[2 * s1 + s2, at, :] * w
                    turns = turns - jnp.round(turns)
                    s, c = sincos(turns)
                    acc[2 * s1 + s2, at, :] += c * real - s * imag

    @pl.loop(0, layers // 2)
    def _(pair):
        for parity in range(2):
            layer_step(pair, parity)

    def mirror(n):
        one = lax.broadcasted_iota(jnp.int32, (n, n), 0)
        two = lax.broadcasted_iota(jnp.int32, (n, n), 1)
        return jnp.where(one + two == n - 1, 1.0, 0.0).astype(BF16)

    flip_c, flip_r = mirror(half_c), mirror(half_r)

    def wide(s1):
        high, mid, low = (dot_nn(part, flip_c) for part in split3(acc[2 * s1 + 1]))
        return jnp.concatenate([(high + mid) + low, acc[2 * s1]], 1)

    high, mid, low = (dot_nn(flip_r, part) for part in split3(wide(1)))
    blocks = half_r // rows_dev
    outb[:blocks] = ((high + mid) + low).reshape(blocks, rows_dev, cols)
    outb[blocks:] = wide(0).reshape(blocks, rows_dev, cols)

    copies = exchange("wa", n_wa, send3, recv3, lambda to: outb.at[to], lambda me: land.at[me])
    land[me_wa] = outb[me_wa]
    noise = jnp.zeros((1, 1), F32)
    for s in range(n_wa):
        noise = noise + gathered[s, layers // 2, 1:2, 0:1]
    scale = lax.rsqrt(noise)
    for copy in copies:
        copy.wait()
    for s in range(n_wa):
        span = slice(s * cols, (s + 1) * cols)
        out_ref[:, span] = land[s] * scale - sky_ref[:, span]


def on_device(grid_cells, visibilities, weights, layer_index, group_index, plane_depths, sky_model):
    n_wa, n_ch = lax.axis_size("wa"), lax.axis_size("ch")
    held = weights.shape[0]
    cap = 2 * held // (n_wa * n_ch)
    rows_dev, columns = sky_model.shape[1:]
    rows = rows_dev * n_wa
    cols = columns // n_wa
    payload = jnp.concatenate(
        [
            visibilities * weights[None],
            grid_cells.astype(F32),
            weights[None],
            group_index.astype(F32)[None],
            layer_index.astype(F32)[None],
            jnp.broadcast_to(plane_depths[None], (1, held)),
        ],
        0,
    )
    vmem = pl.BlockSpec(memory_space=pltpu.VMEM)
    out = pl.pallas_call(
        functools.partial(kernel, (n_wa, n_ch, cap, rows, rows_dev, columns)),
        out_shape=jax.ShapeDtypeStruct((rows_dev, columns), F32),
        in_specs=[vmem, vmem],
        out_specs=vmem,
        scratch_shapes=[
            pltpu.VMEM((n_ch, 8, n_wa * cap), F32),
            pltpu.VMEM((n_ch, 8, n_wa * cap), F32),
            pltpu.VMEM((n_wa, n_wa // 2 + 1, 8, 128), F32),
            pltpu.VMEM((4, rows // 2, cols // 2), F32),
            pltpu.VMEM((2 * rows, n_wa * 128), BF16),
            pltpu.VMEM((cols, n_wa * 128), BF16),
            pltpu.VMEM((2 * rows, cols), F32),
            pltpu.VMEM((4, rows // 2, cols // 2), F32),
            pltpu.VMEM((n_wa, rows_dev, cols), F32),
            pltpu.VMEM((n_wa, rows_dev, cols), F32),
        ]
        + [pltpu.SemaphoreType.DMA((n,)) for n in (n_ch, n_ch, n_wa, n_wa, n_wa, n_wa)],
        compiler_params=pltpu.CompilerParams(
            collective_id=0, has_side_effects=True, vmem_limit_bytes=48 * 1024 * 1024
        ),
    )(payload, sky_model[0])
    return out[None]


def solution(mesh):
    return jax.shard_map(
        on_device,
        mesh=mesh,
        in_specs=(
            P(None, ("wa", "ch")),
            P(None, ("wa", "ch")),
            P(("wa", "ch")),
            P(("wa", "ch")),
            P(("wa", "ch")),
            P("wa"),
            P("ch", "wa", None),
        ),
        out_specs=P("ch", "wa", None),
        check_vma=False,
    )
```

time: 170 us -> 37.8 us (0.22)
  other arithmetic: 92.4 us -> 0.01 us
  Pallas kernels: 0 us -> 33.1 us
  waiting for transfers between devices: 31 us -> 0 us
  between operations: 14.8 us -> 0.69 us
  blocking collectives: 12.6 us -> 0 us
  starting transfers between devices: 7.37 us -> 0 us
  matrix products: 6.98 us -> 0 us
    convert_element_type x5 -> x3, other arithmetic: 74.8 us -> 0.01 us  [the longest x1 0.01 us: on_device(): grid_cells.astype(F32)]
    pallas_call x0 -> x1, Pallas kernels: none -> 33.1 us  [on_device(): pl.pallas_call(functools.partial(kernel, (n_wa, n_ch, cap, rows, rows_dev...]
    reduce_scatter x1 -> x0, waiting for transfers between devices: 24.4 us -> none  [on_device(): lax.psum_scatter(layer_image(row_factors, column_factors, plane_depths[0]...]
    psum x1 -> x0, blocking collectives: 12.6 us -> none  [on_device(): noise_power = lax.psum(jnp.sum(received[2] * received[2]), 'wa')]
    sub x2 -> x0, other arithmetic: 9.59 us -> none  [the longest x1 9.59 us: layer_image(): return jnp.cos(screen) * real_sum - jnp.sin(screen) * imag_sum]
    all_to_all x1 -> x0, starting transfers between devices: 7.33 us -> none  [on_device(): lax.all_to_all(outgoing.reshape(5, dest_count, capacity), ('wa', 'ch'), s...]
    dot_general x1 -> x0, matrix products: 6.98 us -> none  [layer_image(): jnp.dot(row_factors, column_factors, preferred_element_type=jnp.float32)]
    all_to_all x1 -> x0, waiting for transfers between devices: 6.55 us -> none  [on_device(): lax.all_to_all(outgoing.reshape(5, dest_count, capacity), ('wa', 'ch'), s...]
  transfers between devices with their start and end apart: 2 -> 0, of which waited for: 2 -> 0; matrix products, arithmetic and copies ran while one was open for 0% -> 0% of each run, Pallas kernels for 0% -> 0%
where the time goes in v1:
time: 37.8 us; the launch traced here: 37.5 us
  Pallas kernels  33.1 us (88%)
  local copies, waits for them, and re-layouts  3.74 us (10%)
  between operations  0.69 us (2%)
    pallas_call x1, Pallas kernels, on_device(): pl.pallas_call(functools.partial(kernel, (n_wa, n_ch, cap, rows, rows_dev...  33.1 us
    unnamed x13, local copies, waits for them, and re-layouts  3.7 us

profile of v1, /device:TPU:0, one launch (start us, length us, event | category | flops | bytes accessed | tf_op | source)
XLA Modules:
  0.0 37.5 jit_solution(18259177236497311593)
XLA Ops:
  0.7 0.0 copy-start.4
  0.7 0.7 %copy-done.4 = s32[512]{0:T(512)S(1)} copy-done((s32[512]{0:T(512)S(1)}, s32[512]{0:T(512)}, u32[]{:S(2)}) %copy-start.4) | copy-done | bytes 2072
  1.3 0.0 copy-start.5
  1.3 0.0 copy-start.2
  1.3 0.7 %copy-done.5 = s32[512]{0:T(512)S(1)} copy-done((s32[512]{0:T(512)S(1)}, s32[512]{0:T(512)}, u32[]{:S(2)}) %copy-start.5) | copy-done | bytes 2072
  2.0 0.0 copy-done.2
  2.0 0.0 copy-start.1
  2.0 0.0 copy-start.3
  2.0 0.7 %copy-done.1 = f32[512]{0:T(512)S(1)} copy-done((f32[512]{0:T(512)S(1)}, f32[512]{0:T(512)}, u32[]{:S(2)}) %copy-start.1) | copy-done | bytes 2072
  2.7 0.0 copy-done.3
  2.8 0.0 copy-start
  2.8 0.9 %copy-done = f32[1,16,4096]{2,1,0:T(8,128)S(1)} copy-done((f32[1,16,4096]{2,1,0:T(8,128)S(1)}, f32[1,16,4096]{2,1,0:T(8,128)}, u32[]{:S(2)}) %copy-start) | copy-done | bytes 262168
  3.7 33.1 %shard_map.73 = f32[16,4096]{1,0:T(8,128)S(1)} custom-call(f32[8,512]{1,0:T(8,128)S(1)} %concatenate.3.pay_ref, f32[16,4096]{1,0:T(8,128)S(1)} %bitcast.8), custom_call_target="tpu_custom_call" | custom-call | tf_op jit(solution)/shard_map/pallas_call | solution.py:286
  36.8 0.7 %copy.10 = f32[1,16,4096]{2,1,0:T(8,128)} copy(f32[1,16,4096]{2,1,0:T(8,128)S(1)} %bitcast.7) | data formatting | bytes 524288
  (6 shorter events, 0.0 us)
Async XLA Ops:
  0.7 0.7 %copy-start.4 = (s32[512]{0:T(512)S(1)}, s32[512]{0:T(512)}, u32[]{:S(2)}) copy-start(s32[512]{0:T(512)} %param.10) | copy-start | bytes 6148
  1.3 0.7 %copy-start.5 = (s32[512]{0:T(512)S(1)}, s32[512]{0:T(512)}, u32[]{:S(2)}) copy-start(s32[512]{0:T(512)} %param.11) | copy-start | bytes 6148
  1.3 0.7 %copy-start.2 = (s32[2,512]{1,0:T(2,128)S(1)}, s32[2,512]{1,0:T(2,128)}, u32[]{:S(2)}) copy-start(s32[2,512]{1,0:T(2,128)} %param.7) | copy-start | bytes 12292
  2.0 0.7 %copy-start.1 = (f32[512]{0:T(512)S(1)}, f32[512]{0:T(512)}, u32[]{:S(2)}) copy-start(f32[512]{0:T(512)} %param.9) | copy-start | bytes 6148
  2.0 0.7 %copy-start.3 = (f32[2,512]{1,0:T(2,128)S(1)}, f32[2,512]{1,0:T(2,128)}, u32[]{:S(2)}) copy-start(f32[2,512]{1,0:T(2,128)} %param.8) | copy-start | bytes 12292
  2.8 1.0 %copy-start = (f32[1,16,4096]{2,1,0:T(8,128)S(1)}, f32[1,16,4096]{2,1,0:T(8,128)}, u32[]{:S(2)}) copy-start(f32[1,16,4096]{2,1,0:T(8,128)} %param.13) | copy-start | bytes 786436

commit v2 on v1

v2 whole, which is shorter than its diff:
```python
import functools

import jax
import jax.numpy as jnp
from jax import lax
from jax.experimental import pallas as pl
from jax.experimental.pallas import tpu as pltpu
from jax.sharding import PartitionSpec as P

GRID = 8192
MESH = pl.DeviceIdType.MESH
SIN = (3.1415926400772034, -5.167710076668359, 2.5500773865296704, -0.5982904112879445, 0.07765591228493303)
COS = (0.9999999530275129, -4.934792802489486, 4.058410790762989, -1.3318729727896825, 0.21968242357961013)
F32 = jnp.float32
BF16 = jnp.bfloat16


def sincos(turns):
    y = turns * turns
    s = SIN[4]
    c = COS[4]
    for k in (3, 2, 1, 0):
        s = s * y + SIN[k]
        c = c * y + COS[k]
    s = s * turns
    s2 = s + s
    return s2 * c, 1.0 - s2 * s


def wrapped(turns):
    return turns - jnp.round(turns)


def across(index, step):
    moved = 0
    bit = 1
    while bit < 64:
        moved = moved + bit * lax.rem(lax.div(index, bit) + lax.div(step, bit), 2)
        bit *= 2
    return moved


def split3(x):
    high = x.astype(BF16)
    rest = x - high.astype(F32)
    mid = rest.astype(BF16)
    low = (rest - mid.astype(F32)).astype(BF16)
    return high, mid, low


def dot_nt(left, right):
    return lax.dot_general(left, right, (((1,), (1,)), ((), ())), preferred_element_type=F32)


def dot_nn(left, right):
    return jnp.dot(left, right, preferred_element_type=F32)


def remote(axis, step, send_sem, recv_sem, source, target):
    me = lax.axis_index(axis)
    to = across(me, jnp.int32(step))
    return pltpu.make_async_remote_copy(
        src_ref=source(to),
        dst_ref=target(me),
        send_sem=send_sem.at[step],
        recv_sem=recv_sem.at[step],
        device_id={axis: to},
        device_id_type=MESH,
    )


def kernel(
    sizes, cells_in, vis_in, weights_in, layer_in, group_in, depth_in, sky_in, out_ref,
    cells_ref, vis_ref, weights_ref, layer_ref, group_ref, sky_ref,
    msg, got, gathered, depth, a_ref, b_ref, x0_ref, x1_ref, acc, outb, land,
    in_sem, send1, recv1, send2, recv2, send3, recv3,
):
    n_wa, n_ch, cap, rows, rows_dev, columns = sizes
    layers = n_wa
    cols = columns // n_wa
    half_c, half_r = cols // 2, rows // 2
    held = weights_ref.shape[1]
    dests = n_wa * n_ch
    width = layers * cap
    resident = a_ref.shape[0] == layers
    me_wa, me_ch = lax.axis_index("wa"), lax.axis_index("ch")

    loads = [
        pltpu.make_async_copy(source, target, in_sem.at[k])
        for k, (source, target) in enumerate(
            (
                (layer_in, layer_ref), (group_in, group_ref), (weights_in, weights_ref),
                (vis_in, vis_ref), (cells_in, cells_ref), (sky_in, sky_ref),
            )
        )
    ]
    for load in loads:
        load.start()
    barrier = pltpu.get_barrier_semaphore()
    for axis, count, me in (("wa", n_wa, me_wa), ("ch", n_ch, me_ch)):
        for step in range(1, count):
            pl.semaphore_signal(
                barrier, inc=1, device_id={axis: across(me, jnp.int32(step))}, device_id_type=MESH
            )

    earlier = (
        lax.broadcasted_iota(jnp.int32, (held, held), 0)
        < lax.broadcasted_iota(jnp.int32, (held, held), 1)
    )
    earlier = jnp.where(earlier, 1.0, 0.0).astype(BF16)
    for load in loads[:-1]:
        load.wait()
    target = group_ref[...].astype(F32) * float(layers) + layer_ref[...].astype(F32)
    weights = weights_ref[...]
    payload = jnp.concatenate(
        [vis_ref[...] * weights, cells_ref[...].astype(F32), weights, jnp.zeros((3, held), F32)], 0
    )
    onehot = lax.broadcasted_iota(jnp.int32, (dests, held), 0).astype(F32) == target
    before = dot_nn(jnp.where(onehot, 1.0, 0.0).astype(BF16), earlier)
    rank = jnp.sum(jnp.where(onehot, before, 0.0), 0, keepdims=True)
    slot = target * float(cap) + rank
    parts = split3(payload)
    for group in range(n_ch):
        numbers = lax.broadcasted_iota(jnp.int32, (width, held), 0) + group * width
        select = jnp.where(numbers.astype(F32) == slot, 1.0, 0.0).astype(BF16)
        high, mid, low = (dot_nt(part, select) for part in parts)
        msg[group] = (high + mid) + low

    pl.semaphore_wait(barrier, n_wa + n_ch - 2)
    copies = [
        remote("ch", step, send1, recv1, lambda to: msg.at[to], lambda me: got.at[me])
        for step in range(1, n_ch)
    ]
    for copy in copies:
        copy.start()
    got[me_ch] = msg[me_ch]

    left = me_wa * cols - columns // 2 + GRID // 8 + half_c
    top = GRID // 8

    @pl.loop(0, half_r // 8)
    def _(i):
        p = lax.broadcasted_iota(jnp.int32, (8, half_c), 0) + i * 8
        q = lax.broadcasted_iota(jnp.int32, (8, half_c), 1)
        at = pl.ds(pl.multiple_of(i * 8, 8), 8)
        for s1 in range(2):
            for s2 in range(2):
                l_pix = top + p if s1 == 0 else top - 1 - p
                m_pix = left + q if s2 == 0 else left - 1 - q
                l = 0.8 * l_pix.astype(F32) / GRID
                m = 0.8 * m_pix.astype(F32) / GRID
                s = l * l + m * m
                depth[2 * s1 + s2, at, :] = -s / (1.0 + jnp.sqrt(1.0 - s))
                acc[2 * s1 + s2, at, :] = jnp.zeros((8, half_c), F32)

    for copy in copies:
        copy.wait()

    lane = lax.broadcasted_iota(jnp.int32, (8, 128), 1)
    sub = lax.broadcasted_iota(jnp.int32, (8, 128), 0)

    def packed(layer):
        tile = jnp.zeros((8, 128), F32)
        at = layer * cap
        for c in range(n_ch):
            piece = got[c, :, at // 128 * 128 : at // 128 * 128 + 128]
            shift = (c * cap - at) % 128
            if shift:
                piece = pltpu.roll(piece, shift, 1)
            tile = jnp.where((lane >= c * cap) & (lane < (c + 1) * cap), piece, tile)
        return tile

    for pair in range(layers // 2):
        odd = pltpu.roll(packed(2 * pair + 1), 4, 0)
        gathered[me_wa, pair] = jnp.where(sub < 4, packed(2 * pair), odd)
    power = jnp.zeros((1, width), F32)
    for c in range(n_ch):
        weight = got[c, 4:5, :]
        power = power + weight * weight
    power = jnp.sum(power, 1, keepdims=True)
    gathered[me_wa, layers // 2] = jnp.where(sub == 0, depth_in[0], jnp.where(sub == 1, power, 0.0))

    def spread(step):
        return remote("wa", step, send2, recv2, lambda to: gathered.at[me_wa], lambda me: gathered.at[me])

    for step in range(1, n_wa):
        spread(step).start()

    scale = 0.5 / GRID
    fine = (sub * 2 + 1).astype(F32) * scale
    coarse = (sub * 32).astype(F32) * scale
    center_c = 2 * left - 1
    center_high = lax.div(center_c + 2 * GRID, 64) - GRID // 32
    center_low = center_c - 64 * center_high
    center_high = center_high.astype(F32) * (64 * scale)
    center_low = center_low.astype(F32) * scale

    def rowwise(*values):
        tile = jnp.zeros((8, 128), F32)
        for row, value in values:
            tile = jnp.where(sub == row, value, tile)
        return tile

    mixed_u = rowwise((0, (GRID // 4 - 1) * scale), (1, 16 * scale), (3, 256 * scale))
    mixed_v = rowwise((0, center_high), (2, 16 * scale), (4, 256 * scale))
    mixed_low = rowwise((0, center_low))

    def times(first, second):
        (s1, c1), (s2, c2) = first, second
        return s1 * c2 + c1 * s2, c1 * c2 - s1 * s2

    def tables(block, pair, parity, held_at):
        lanes = pl.ds(pl.multiple_of(block * 128, 128), 128)
        base = 4 * parity
        zr, zi, u, v = (gathered[block, pair, base + k : base + k + 1, :] for k in range(4))
        ub, vb = jnp.broadcast_to(u, (8, 128)), jnp.broadcast_to(v, (8, 128))
        ms, mc = sincos(wrapped(wrapped(ub * mixed_u) + wrapped(vb * mixed_v) + vb * mixed_low))
        row = lambda k: (ms[k : k + 1, :], mc[k : k + 1, :])
        sc, cc = row(0)
        wr, wi = zr * cc - zi * sc, zr * sc + zi * cc
        wr, wi = jnp.broadcast_to(wr, (16, 128)), jnp.broadcast_to(wi, (16, 128))
        for cell, half, up, far in ((ub, half_r, 1, 3), (vb, half_c, 2, 4)):
            near = sincos(wrapped(cell * fine))
            upper = times(near, row(up))
            fs, fc = (jnp.concatenate([near[k], upper[k]], 0) for k in range(2))
            ladder = [sincos(wrapped(cell * coarse))]
            if half > 128:
                ladder.append(times(ladder[0], row(far)))
            for a in range(half // 16):
                es, ec = ladder[a // 8]
                e = es[a % 8 : a % 8 + 1, :], ec[a % 8 : a % 8 + 1, :]
                s, c = times(e, (fs, fc))
                if up == 1:
                    for k, term in enumerate((wr * c, wr * s, wi * c, wi * s)):
                        a_ref[held_at, k * half + 16 * a : k * half + 16 * a + 16, lanes] = term.astype(BF16)
                else:
                    for k, term in enumerate((c, s)):
                        b_ref[held_at, k * half + 16 * a : k * half + 16 * a + 16, lanes] = term.astype(BF16)

    def products(held_at, x_ref):
        deep = min(1024, n_wa * 128)
        for i in range(4 * half_r // 256):
            tall = slice(i * 256, i * 256 + 256)
            if n_wa * 128 == deep:
                x_ref[tall, :] = dot_nt(a_ref[held_at, tall, :], b_ref[held_at])
            else:
                x_ref[tall, :] = jnp.zeros((256, cols), F32)

                @pl.loop(0, n_wa * 128 // deep)
                def _(k):
                    inner = pl.ds(pl.multiple_of(k * deep, deep), deep)
                    x_ref[tall, :] += dot_nt(a_ref[held_at, tall, inner], b_ref[held_at, :, inner])

    def screened(x_ref, layer, i):
        w = gathered[layer, layers // 2, 0:1, 0:1]
        x = [
            [x_ref[k * half_r + i * 8 : k * half_r + i * 8 + 8, g * half_c : (g + 1) * half_c] for g in range(2)]
            for k in range(4)
        ]
        (rcc, rcs), (rsc, rss), (icc, ics), (isc, iss) = x
        same_r, cross_r = (rcc - rss, rcc + rss), (isc + ics, isc - ics)
        same_i, cross_i = (icc - iss, icc + iss), (rsc + rcs, rsc - rcs)
        at = slice(i * 8, i * 8 + 8)
        for s1 in range(2):
            for s2 in range(2):
                k = 0 if s1 == s2 else 1
                if s1 == 0:
                    real, imag = same_r[k] - cross_r[k], same_i[k] + cross_i[k]
                else:
                    real, imag = same_r[k] + cross_r[k], same_i[k] - cross_i[k]
                s, c = sincos(wrapped(depth[2 * s1 + s2, at, :] * w))
                acc[2 * s1 + s2, at, :] += c * real - s * imag

    def screen(x_ref, layer):
        for i in range(half_r // 8):
            screened(x_ref, layer, i)

    if resident:

        @pl.loop(0, n_wa)
        def _(step):
            @pl.when(step > 0)
            def _():
                spread(step).wait_recv()

            block = across(me_wa, step)

            @pl.loop(0, layers // 2)
            def _(pair):
                for parity in range(2):
                    tables(block, pair, parity, 2 * pair + parity)

        x1_ref[...] = jnp.zeros_like(x1_ref)

        @pl.loop(0, layers // 2)
        def _(pair):
            products(2 * pair, x0_ref)
            screen(x1_ref, jnp.maximum(2 * pair - 1, 0))
            products(2 * pair + 1, x1_ref)
            screen(x0_ref, 2 * pair)

        screen(x1_ref, layers - 1)
    else:
        for step in range(1, n_wa):
            spread(step).wait_recv()

        @pl.loop(0, layers // 2)
        def _(pair):
            for parity in range(2):

                @pl.loop(0, n_wa)
                def _(block):
                    tables(block, pair, parity, 0)

                products(0, x0_ref)
                screen(x0_ref, 2 * pair + parity)

    def mirror(n):
        one = lax.broadcasted_iota(jnp.int32, (n, n), 0)
        two = lax.broadcasted_iota(jnp.int32, (n, n), 1)
        return jnp.where(one + two == n - 1, 1.0, 0.0).astype(BF16)

    flip_c, flip_r = mirror(half_c), mirror(half_r)

    def wide(s1):
        high, mid, low = (dot_nn(part, flip_c) for part in split3(acc[2 * s1 + 1]))
        return jnp.concatenate([(high + mid) + low, acc[2 * s1]], 1)

    high, mid, low = (dot_nn(flip_r, part) for part in split3(wide(1)))
    blocks = half_r // rows_dev
    outb[:blocks] = ((high + mid) + low).reshape(blocks, rows_dev, cols)
    outb[blocks:] = wide(0).reshape(blocks, rows_dev, cols)

    copies = [
        remote("wa", step, send3, recv3, lambda to: outb.at[to], lambda me: land.at[me])
        for step in range(1, n_wa)
    ]
    for copy in reversed(copies):
        copy.start()
    land[me_wa] = outb[me_wa]
    noise = jnp.zeros((1, 1), F32)
    for s in range(n_wa):
        noise = noise + gathered[s, layers // 2, 1:2, 0:1]
    factor = lax.rsqrt(noise)
    for step in range(1, n_wa):
        spread(step).wait_send()
    loads[-1].wait()
    for copy in copies:
        copy.wait()
    for s in range(n_wa):
        span = slice(s * cols, (s + 1) * cols)
        out_ref[:, span] = land[s] * factor - sky_ref[:, span]


def on_device(grid_cells, visibilities, weights, layer_index, group_index, plane_depths, sky_model):
    n_wa, n_ch = lax.axis_size("wa"), lax.axis_size("ch")
    held = weights.shape[0]
    cap = 2 * held // (n_wa * n_ch)
    rows_dev, columns = sky_model.shape[1:]
    rows = rows_dev * n_wa
    cols = columns // n_wa
    depth = n_wa * 128
    table = 2 * (2 * rows + cols) * depth
    kept = n_wa if n_wa * table <= 16 * 1024 * 1024 else 1
    vmem = pl.BlockSpec(memory_space=pltpu.VMEM)
    hbm = pl.BlockSpec(memory_space=pltpu.HBM)
    smem = pl.BlockSpec(memory_space=pltpu.SMEM)
    out = pl.pallas_call(
        functools.partial(kernel, (n_wa, n_ch, cap, rows, rows_dev, columns)),
        out_shape=jax.ShapeDtypeStruct((rows_dev, columns), F32),
        in_specs=[hbm, hbm, hbm, hbm, hbm, smem, hbm],
        out_specs=vmem,
        scratch_shapes=[
            pltpu.VMEM((2, held), jnp.int32),
            pltpu.VMEM((2, held), F32),
            pltpu.VMEM((1, held), F32),
            pltpu.VMEM((1, held), jnp.int32),
            pltpu.VMEM((1, held), jnp.int32),
            pltpu.VMEM((rows_dev, columns), F32),
            pltpu.VMEM((n_ch, 8, n_wa * cap), F32),
            pltpu.VMEM((n_ch, 8, n_wa * cap), F32),
            pltpu.VMEM((n_wa, n_wa // 2 + 1, 8, 128), F32),
            pltpu.VMEM((4, rows // 2, cols // 2), F32),
            pltpu.VMEM((kept, 2 * rows, depth), BF16),
            pltpu.VMEM((kept, cols, depth), BF16),
            pltpu.VMEM((2 * rows, cols), F32),
            pltpu.VMEM((2 * rows, cols), F32),
            pltpu.VMEM((4, rows // 2, cols // 2), F32),
            pltpu.VMEM((n_wa, rows_dev, cols), F32),
            pltpu.VMEM((n_wa, rows_dev, cols), F32),
        ]
        + [pltpu.SemaphoreType.DMA((n,)) for n in (6, n_ch, n_ch, n_wa, n_wa, n_wa, n_wa)],
        compiler_params=pltpu.CompilerParams(
            collective_id=0, has_side_effects=True, vmem_limit_bytes=36 * 1024 * 1024
        ),
    )(
        grid_cells, visibilities, weights[None], layer_index[None], group_index[None],
        plane_depths, sky_model[0],
    )
    return out[None]


def solution(mesh):
    return jax.shard_map(
        on_device,
        mesh=mesh,
        in_specs=(
            P(None, ("wa", "ch")),
            P(None, ("wa", "ch")),
            P(("wa", "ch")),
            P(("wa", "ch")),
            P(("wa", "ch")),
            P("wa"),
            P("ch", "wa", None),
        ),
        out_specs=P("ch", "wa", None),
        check_vma=False,
    )
```

time: 37.8 us -> 32 us (0.85)
  Pallas kernels: 33.1 us -> 26.7 us
  local copies, waits for them, and re-layouts: 3.74 us -> 4.38 us
    pallas_call x1, Pallas kernels: 33.1 us -> 26.7 us  [on_device(): pl.pallas_call(functools.partial(kernel, (n_wa, n_ch, cap, rows, rows_dev...]
    unnamed x13, local copies, waits for them, and re-layouts: 3.7 us -> 4.38 us
where the time goes in v2:
time: 32 us; the launch traced here: 31.7 us
  Pallas kernels  26.7 us (83%)
  local copies, waits for them, and re-layouts  4.38 us (14%)
  between operations  0.69 us (2%)
    pallas_call x1, Pallas kernels, on_device(): pl.pallas_call(functools.partial(kernel, (n_wa, n_ch, cap, rows, rows_dev...  26.7 us
    unnamed x13, local copies, waits for them, and re-layouts  4.38 us

profile of v2, /device:TPU:0, one launch (start us, length us, event | category | flops | bytes accessed | tf_op | source)
XLA Modules:
  0.0 31.7 jit_solution(1339857292300149451)
XLA Ops:
  0.0 0.0 copy-start.2
  0.7 0.0 copy-start.1
  0.7 0.0 copy-done.2
  0.7 0.7 %copy-done.1 = s32[2,512]{1,0:T(2,128)S(1)} copy-done((s32[2,512]{1,0:T(2,128)S(1)}, s32[2,512]{1,0:T(2,128)}, u32[]{:S(2)}) %copy-start.1) | copy-done | bytes 4120
  1.4 0.0 copy-start
  1.4 0.9 %copy-done = f32[1,16,4096]{2,1,0:T(8,128)S(1)} copy-done((f32[1,16,4096]{2,1,0:T(8,128)S(1)}, f32[1,16,4096]{2,1,0:T(8,128)}, u32[]{:S(2)}) %copy-start) | copy-done | bytes 262168
  2.3 0.0 copy-start.3
  2.3 0.7 %copy-done.3 = f32[512]{0:T(512)S(1)} copy-done((f32[512]{0:T(512)S(1)}, f32[512]{0:T(512)}, u32[]{:S(2)}) %copy-start.3) | copy-done | bytes 2072
  3.0 0.0 copy-start.4
  3.0 0.7 %copy-done.4 = s32[512]{0:T(512)S(1)} copy-done((s32[512]{0:T(512)S(1)}, s32[512]{0:T(512)}, u32[]{:S(2)}) %copy-start.4) | copy-done | bytes 2072
  3.7 0.0 copy-start.5
  3.7 0.7 %copy-done.5 = s32[512]{0:T(512)S(1)} copy-done((s32[512]{0:T(512)S(1)}, s32[512]{0:T(512)}, u32[]{:S(2)}) %copy-start.5) | copy-done | bytes 2072
  4.4 26.7 %shard_map.73 = f32[16,4096]{1,0:T(8,128)S(1)} custom-call(s32[2,512]{1,0:T(2,128)S(1)} %copy-done.1, f32[2,512]{1,0:T(2,128)S(1)} %copy-done.2, f32[1,512]{1,0:T(1,128)S(1)} %bitcast.7, s32[1,512]{1,0:T(1,128)S(1)} %bitcast.8, s32[1,512]{1,0:T(1,128)S(1)} %bitcast.9, f32[1]{0:T(128)S(6)} %copy.9.depth_in, f32[16,4096]{1,0:T(8,128)S(1)} %bitcast.6), custom_call_target="tpu_custom_call" | custom-call | tf_op jit(solution)/shard_map/pallas_call | solution.py:368
  31.0 0.7 %copy.10 = f32[1,16,4096]{2,1,0:T(8,128)} copy(f32[1,16,4096]{2,1,0:T(8,128)S(1)} %bitcast.5) | data formatting | bytes 524288
Async XLA Ops:
  0.0 0.7 %copy-start.2 = (f32[2,512]{1,0:T(2,128)S(1)}, f32[2,512]{1,0:T(2,128)}, u32[]{:S(2)}) copy-start(f32[2,512]{1,0:T(2,128)} %vis_in.1) | copy-start | bytes 12292
  0.7 0.7 %copy-start.1 = (s32[2,512]{1,0:T(2,128)S(1)}, s32[2,512]{1,0:T(2,128)}, u32[]{:S(2)}) copy-start(s32[2,512]{1,0:T(2,128)} %cells_in.1) | copy-start | bytes 12292
  1.4 0.9 %copy-start = (f32[1,16,4096]{2,1,0:T(8,128)S(1)}, f32[1,16,4096]{2,1,0:T(8,128)}, u32[]{:S(2)}) copy-start(f32[1,16,4096]{2,1,0:T(8,128)} %param.13) | copy-start | bytes 786436
  2.3 0.7 %copy-start.3 = (f32[512]{0:T(512)S(1)}, f32[512]{0:T(512)}, u32[]{:S(2)}) copy-start(f32[512]{0:T(512)} %param.9) | copy-start | bytes 6148
  3.0 0.7 %copy-start.4 = (s32[512]{0:T(512)S(1)}, s32[512]{0:T(512)}, u32[]{:S(2)}) copy-start(s32[512]{0:T(512)} %param.10) | copy-start | bytes 6148
  3.7 0.7 %copy-start.5 = (s32[512]{0:T(512)S(1)}, s32[512]{0:T(512)}, u32[]{:S(2)}) copy-start(s32[512]{0:T(512)} %param.11) | copy-start | bytes 6148

commit v3 on v2

--- a/solution.py
+++ b/solution.py
@@ -79,6 +79,8 @@
     layers = n_wa
     cols = columns // n_wa
     half_c, half_r = cols // 2, rows // 2
+    chunks = outb.shape[0]
+    chunk = half_c // chunks
     held = weights_ref.shape[1]
     dests = n_wa * n_ch
     width = layers * cap
@@ -234,46 +236,73 @@
                     for k, term in enumerate((wr * c, wr * s, wi * c, wi * s)):
                         a_ref[held_at, k * half + 16 * a : k * half + 16 * a + 16, lanes] = term.astype(BF16)
                 else:
+                    at = 2 * chunk * (16 * a // chunk) + 16 * a % chunk
                     for k, term in enumerate((c, s)):
-                        b_ref[held_at, k * half + 16 * a : k * half + 16 * a + 16, lanes] = term.astype(BF16)
-
-    def products(held_at, x_ref):
+                        b_ref[held_at, at + k * chunk : at + k * chunk + 16, lanes] = term.astype(BF16)
+
+    def products(held_at, x_ref, h):
         deep = min(1024, n_wa * 128)
+        across_h = slice(2 * chunk * h, 2 * chunk * (h + 1))
         for i in range(4 * half_r // 256):
             tall = slice(i * 256, i * 256 + 256)
             if n_wa * 128 == deep:
-                x_ref[tall, :] = dot_nt(a_ref[held_at, tall, :], b_ref[held_at])
+                x_ref[tall, :] = dot_nt(a_ref[held_at, tall, :], b_ref[held_at, across_h, :])
             else:
-                x_ref[tall, :] = jnp.zeros((256, cols), F32)
+                x_ref[tall, :] = jnp.zeros((256, 2 * chunk), F32)
 
                 @pl.loop(0, n_wa * 128 // deep)
                 def _(k):
                     inner = pl.ds(pl.multiple_of(k * deep, deep), deep)
-                    x_ref[tall, :] += dot_nt(a_ref[held_at, tall, inner], b_ref[held_at, :, inner])
-
-    def screened(x_ref, layer, i):
+                    x_ref[tall, :] += dot_nt(a_ref[held_at, tall, inner], b_ref[held_at, across_h, inner])
+
+    def screen(x_ref, layer, h):
         w = gathered[layer, layers // 2, 0:1, 0:1]
-        x = [
-            [x_ref[k * half_r + i * 8 : k * half_r + i * 8 + 8, g * half_c : (g + 1) * half_c] for g in range(2)]
-            for k in range(4)
+        wide_at = slice(chunk * h, chunk * (h + 1))
+        for i in range(half_r // 8):
+            x = [
+                [x_ref[k * half_r + i * 8 : k * half_r + i * 8 + 8, g * chunk : (g + 1) * chunk] for g in range(2)]
+                for k in range(4)
+            ]
+            (rcc, rcs), (rsc, rss), (icc, ics), (isc, iss) = x
+            same_r, cross_r = (rcc - rss, rcc + rss), (isc + ics, isc - ics)
+            same_i, cross_i = (icc - iss, icc + iss), (rsc + rcs, rsc - rcs)
+            at = slice(i * 8, i * 8 + 8)
+            for s1 in range(2):
+                for s2 in range(2):
+                    k = 0 if s1 == s2 else 1
+                    if s1 == 0:
+                        real, imag = same_r[k] - cross_r[k], same_i[k] + cross_i[k]
+                    else:
+                        real, imag = same_r[k] + cross_r[k], same_i[k] - cross_i[k]
+                    s, c = sincos(wrapped(depth[2 * s1 + s2, at, wide_at] * w))
+                    acc[2 * s1 + s2, at, wide_at] += c * real - s * imag
+
+    def mirror(n):
+        one = lax.broadcasted_iota(jnp.int32, (n, n), 0)
+        two = lax.broadcasted_iota(jnp.int32, (n, n), 1)
+        return jnp.where(one + two == n - 1, 1.0, 0.0).astype(BF16)
+
+    flip_c, flip_r = mirror(chunk), mirror(half_r)
+    blocks = half_r // rows_dev
+
+    def wide(s1, h):
+        wide_at = slice(chunk * h, chunk * (h + 1))
+        high, mid, low = (dot_nn(part, flip_c) for part in split3(acc[2 * s1 + 1, :, wide_at]))
+        return jnp.concatenate([(high + mid) + low, acc[2 * s1, :, wide_at]], 1)
+
+    def owned(h):
+        return [
+            remote("wa", step, send3.at[h], recv3.at[h], lambda to: outb.at[h, to], lambda me: land.at[h, me])
+            for step in range(1, n_wa)
         ]
-        (rcc, rcs), (rsc, rss), (icc, ics), (isc, iss) = x
-        same_r, cross_r = (rcc - rss, rcc + rss), (isc + ics, isc - ics)
-        same_i, cross_i = (icc - iss, icc + iss), (rsc + rcs, rsc - rcs)
-        at = slice(i * 8, i * 8 + 8)
-        for s1 in range(2):
-            for s2 in range(2):
-                k = 0 if s1 == s2 else 1
-                if s1 == 0:
-                    real, imag = same_r[k] - cross_r[k], same_i[k] + cross_i[k]
-                else:
-                    real, imag = same_r[k] + cross_r[k], same_i[k] - cross_i[k]
-                s, c = sincos(wrapped(depth[2 * s1 + s2, at, :] * w))
-                acc[2 * s1 + s2, at, :] += c * real - s * imag
-
-    def screen(x_ref, layer):
-        for i in range(half_r // 8):
-            screened(x_ref, layer, i)
+
+    def hand_over(h):
+        high, mid, low = (dot_nn(flip_r, part) for part in split3(wide(1, h)))
+        outb[h, :blocks] = ((high + mid) + low).reshape(blocks, rows_dev, 2 * chunk)
+        outb[h, blocks:] = wide(0, h).reshape(blocks, rows_dev, 2 * chunk)
+        for copy in reversed(owned(h)):
+            copy.start()
+        land[h, me_wa] = outb[h, me_wa]
 
     if resident:
 
@@ -290,16 +319,18 @@
                 for parity in range(2):
                     tables(block, pair, parity, 2 * pair + parity)
 
-        x1_ref[...] = jnp.zeros_like(x1_ref)
-
-        @pl.loop(0, layers // 2)
-        def _(pair):
-            products(2 * pair, x0_ref)
-            screen(x1_ref, jnp.maximum(2 * pair - 1, 0))
-            products(2 * pair + 1, x1_ref)
-            screen(x0_ref, 2 * pair)
-
-        screen(x1_ref, layers - 1)
+        for h in range(chunks):
+            x1_ref[...] = jnp.zeros_like(x1_ref)
+
+            @pl.loop(0, layers // 2)
+            def _(pair):
+                products(2 * pair, x0_ref, h)
+                screen(x1_ref, jnp.maximum(2 * pair - 1, 0), h)
+                products(2 * pair + 1, x1_ref, h)
+                screen(x0_ref, 2 * pair, h)
+
+            screen(x1_ref, layers - 1, h)
+            hand_over(h)
     else:
         for step in range(1, n_wa):
             spread(step).wait_recv()
@@ -312,32 +343,13 @@
                 def _(block):
                     tables(block, pair, parity, 0)
 
-                products(0, x0_ref)
-                screen(x0_ref, 2 * pair + parity)
-
-    def mirror(n):
-        one = lax.broadcasted_iota(jnp.int32, (n, n), 0)
-        two = lax.broadcasted_iota(jnp.int32, (n, n), 1)
-        return jnp.where(one + two == n - 1, 1.0, 0.0).astype(BF16)
-
-    flip_c, flip_r = mirror(half_c), mirror(half_r)
-
-    def wide(s1):
-        high, mid, low = (dot_nn(part, flip_c) for part in split3(acc[2 * s1 + 1]))
-        return jnp.concatenate([(high + mid) + low, acc[2 * s1]], 1)
-
-    high, mid, low = (dot_nn(flip_r, part) for part in split3(wide(1)))
-    blocks = half_r // rows_dev
-    outb[:blocks] = ((high + mid) + low).reshape(blocks, rows_dev, cols)
-    outb[blocks:] = wide(0).reshape(blocks, rows_dev, cols)
-
-    copies = [
-        remote("wa", step, send3, recv3, lambda to: outb.at[to], lambda me: land.at[me])
-        for step in range(1, n_wa)
-    ]
-    for copy in reversed(copies):
-        copy.start()
-    land[me_wa] = outb[me_wa]
+                for h in range(chunks):
+                    products(0, x0_ref, h)
+                    screen(x0_ref, 2 * pair + parity, h)
+
+        for h in range(chunks):
+            hand_over(h)
+
     noise = jnp.zeros((1, 1), F32)
     for s in range(n_wa):
         noise = noise + gathered[s, layers // 2, 1:2, 0:1]
@@ -345,11 +357,19 @@
     for step in range(1, n_wa):
         spread(step).wait_send()
     loads[-1].wait()
-    for copy in copies:
-        copy.wait()
-    for s in range(n_wa):
-        span = slice(s * cols, (s + 1) * cols)
-        out_ref[:, span] = land[s] * factor - sky_ref[:, span]
+    for h in range(chunks):
+        for copy in owned(h):
+            copy.wait()
+        for s in range(n_wa):
+            minus = s * cols + half_c - chunk * (h + 1)
+            plus = s * cols + half_c + chunk * h
+            if chunk % 128:
+                span = slice(s * cols, (s + 1) * cols)
+                out_ref[:, span] = land[h, s] * factor - sky_ref[:, span]
+            else:
+                for k, at in enumerate((minus, plus)):
+                    span = slice(at, at + chunk)
+                    out_ref[:, span] = land[h, s, :, k * chunk : (k + 1) * chunk] * factor - sky_ref[:, span]
 
 
 def on_device(grid_cells, visibilities, weights, layer_index, group_index, plane_depths, sky_model):
@@ -362,6 +382,7 @@
     depth = n_wa * 128
     table = 2 * (2 * rows + cols) * depth
     kept = n_wa if n_wa * table <= 16 * 1024 * 1024 else 1
+    chunks = max(1, cols // 256)
     vmem = pl.BlockSpec(memory_space=pltpu.VMEM)
     hbm = pl.BlockSpec(memory_space=pltpu.HBM)
     smem = pl.BlockSpec(memory_space=pltpu.SMEM)
@@ -383,15 +404,16 @@
             pltpu.VMEM((4, rows // 2, cols // 2), F32),
             pltpu.VMEM((kept, 2 * rows, depth), BF16),
             pltpu.VMEM((kept, cols, depth), BF16),
-            pltpu.VMEM((2 * rows, cols), F32),
-            pltpu.VMEM((2 * rows, cols), F32),
+            pltpu.VMEM((2 * rows, cols // chunks), F32),
+            pltpu.VMEM((2 * rows, cols // chunks), F32),
             pltpu.VMEM((4, rows // 2, cols // 2), F32),
-            pltpu.VMEM((n_wa, rows_dev, cols), F32),
-            pltpu.VMEM((n_wa, rows_dev, cols), F32),
+            pltpu.VMEM((chunks, n_wa, rows_dev, cols // chunks), F32),
+            pltpu.VMEM((chunks, n_wa, rows_dev, cols // chunks), F32),
         ]
-        + [pltpu.SemaphoreType.DMA((n,)) for n in (6, n_ch, n_ch, n_wa, n_wa, n_wa, n_wa)],
+        + [pltpu.SemaphoreType.DMA((n,)) for n in (6, n_ch, n_ch, n_wa, n_wa)]
+        + [pltpu.SemaphoreType.DMA((chunks, n_wa))] * 2,
         compiler_params=pltpu.CompilerParams(
-            collective_id=0, has_side_effects=True, vmem_limit_bytes=36 * 1024 * 1024
+            collective_id=0, has_side_effects=True, vmem_limit_bytes=56 * 1024 * 1024
         ),
     )(
         grid_cells, visibilities, weights[None], layer_index[None], group_index[None],

time: 32 us -> 30.4 us (0.950)
  local copies, waits for them, and re-layouts: 4.38 us -> 1.67 us
  Pallas kernels: 26.7 us -> 27.9 us
    unnamed x13 -> x1, local copies, waits for them, and re-layouts: 4.38 us -> 1.67 us
    pallas_call x1, Pallas kernels: 26.7 us -> 27.9 us  [on_device(): pl.pallas_call(functools.partial(kernel, (n_wa, n_ch, cap, rows, rows_dev...]
where the time goes in v3:
time: 30.4 us; the launch traced here: 30.2 us
  Pallas kernels  27.9 us (92%)
  local copies, waits for them, and re-layouts  1.67 us (5%)
  between operations  0.66 us (2%)
    pallas_call x1, Pallas kernels, on_device(): pl.pallas_call(functools.partial(kernel, (n_wa, n_ch, cap, rows, rows_dev...  27.9 us
    unnamed x1, local copies, waits for them, and re-layouts  1.67 us

profile of v3, /device:TPU:0, one launch (start us, length us, event | category | flops | bytes accessed | tf_op | source)
XLA Modules:
  0.0 30.2 jit_solution(2207529373196759050)
XLA Ops:
  0.7 27.9 %shard_map.73 = f32[16,4096]{1,0:T(8,128)} custom-call(s32[2,512]{1,0:T(2,128)} %cells_in.1, f32[2,512]{1,0:T(2,128)} %vis_in.1, f32[1,512]{1,0:T(1,128)} %bitcast.7, s32[1,512]{1,0:T(1,128)} %bitcast.8, s32[1,512]{1,0:T(1,128)} %bitcast.9, f32[1]{0:T(128)S(6)} %copy.9.depth_in, f32[16,4096]{1,0:T(8,128)} %bitcast.6), custom_call_target="tpu_custom_call" | custom-call | tf_op jit(solution)/shard_map/pallas_call | solution.py:389
  28.5 1.7 %copy.10 = f32[1,16,4096]{2,1,0:T(8,128)} copy(f32[1,16,4096]{2,1,0:T(8,128)} %bitcast.5) | data formatting | bytes 524288
